TPU v7x, 32 devices: a whole 2x2x4 slice. The times are simulated.
32 devices in a mesh: col: 4 (over y, core), row: 8 (over z, x).
Axes of the slice: x: 2, y: 2, z: 4, core: 2. Of those that a mesh axis runs over, the one named last changes fastest.
Arguments:
- column_table: float32 [32768, 512], P('row', 'col'), may hold values from -3 to 3
- bag_rows: int32 [256, 32], P('row'), may hold values from 0 to 32767
Outputs:
- row_table: float32 [8, 4096, 512], P(None, ('col', 'row'))
- pooled: float32 [256, 512], P('row', 'col')
Inputs may be any that keep to these rules, and one draw needn't show every extreme that they name: `bag_rows`: row indices of the table; a few rows are named far more often than the rest.
All inputs are finite; a program needn't handle non-finite values.
Results may differ from a plain program's by a relative error of at most 0.000078.
Values sent between devices are 32-bit elements; how exact they have to be, the bound alone decides.
A program may use at most 64 MiB of HBM per device.

v0:
```python
import functools
import math

import jax
import jax.numpy as jnp
from jax import lax
from jax.experimental import pallas as pl
from jax.experimental.pallas import tpu as pltpu
from jax.sharding import PartitionSpec as P

MESH = pl.DeviceIdType.MESH
LANES = 128
SUBLANES = 8


def pooling(positions, table_rows):
    row_count = table_rows.shape[0]
    bag_count = positions.shape[0]
    block_rows = math.gcd(row_count, 512)
    turns = row_count // block_rows
    running = jnp.zeros((bag_count, table_rows.shape[1]), jnp.float32)
    tile_ids = jnp.arange(block_rows, dtype=jnp.int32)

    def advance(turn, carried):
        offset = turn * block_rows
        within = positions - offset
        matches = within[:, :, None] == tile_ids[None, None, :]
        counts = jnp.sum(matches.astype(jnp.float32), axis=1)
        table_block = lax.dynamic_slice_in_dim(table_rows, offset, block_rows, 0)
        return carried + jnp.dot(
            counts, table_block, precision=lax.Precision.HIGHEST, preferred_element_type=jnp.float32
        )

    return lax.fori_loop(0, turns, advance, running)


def general(column_table, bag_rows):
    row_groups = lax.axis_size("row")
    col_groups = lax.axis_size("col")
    block_len, col_width = column_table.shape
    full_width = col_width * col_groups
    span = block_len // (col_groups * row_groups)
    row_index = lax.axis_index("row")
    every_bag = lax.all_gather(bag_rows, "row", axis=0, tiled=True)
    sectioned = column_table.reshape(col_groups, row_groups, span, col_width)
    moved = lax.all_to_all(
        lax.all_to_all(sectioned, "col", split_axis=0, concat_axis=3, tiled=True),
        "row",
        split_axis=1,
        concat_axis=0,
        tiled=True,
    )
    row_table = moved.reshape(row_groups, span, full_width)
    first_row = row_index * block_len
    shifted = every_bag - first_row
    inside = (shifted >= 0) & (shifted < block_len)
    positions = jnp.where(inside, shifted, -1)
    pooled = lax.psum_scatter(
        pooling(positions, column_table), "row", scatter_dimension=0, tiled=True
    )
    return (row_table, pooled)


def flipped(index, mask, count):
    result, bit = 0, 1
    while bit < count:
        digit = lax.rem(lax.div(index, bit), 2)
        result = result + (1 - digit if mask & bit else digit) * bit
        bit *= 2
    return result


def kernel(
    row_groups, col_groups,
    table_ref, bags_ref, out_ref, pooled_ref,
    table_v, bags_v, packed, gathered, counts, partial, arrived, halves, crossed,
    load_sem, bag_sem, own_sem, send_sem, recv_sem, bag_send, bag_recv, sum_send, sum_recv, cross_send, cross_recv,
):
    rows, cols = row_groups, col_groups
    r, c = lax.axis_index("row"), lax.axis_index("col")
    block_len, width = table_ref.shape
    span = block_len // (rows * cols)
    own_bags, bag_len = bags_ref.shape
    per_vreg = LANES // bag_len
    flat = c * rows + r

    bag_load = pltpu.make_async_copy(bags_ref, bags_v, bag_sem)
    bag_load.start()
    load = pltpu.make_async_copy(table_ref, table_v, load_sem)
    load.start()
    own = pltpu.make_async_copy(
        table_ref.at[pl.ds(flat * span, span), :],
        out_ref.at[r, c],
        own_sem,
    )
    own.start()

    masks = [(mr, mc) for mr in range(rows) for mc in range(cols) if (mr, mc) != (0, 0)]
    half = rows // 2
    far = [m for m in masks if m[0] >= half]
    near = sorted((m for m in masks if m[0] < half), key=lambda m: -m[0])
    far = sorted(far, key=lambda m: (m[0] >= half + half // 2, m[1], m[0]))
    order = [m for pair in zip(far, near + [None]) for m in pair if m]
    cuts = [len(order) * n // 31 for n in CUTS]

    def peer(mr, mc):
        return flipped(r, mr, rows), flipped(c, mc, cols)

    barrier = pltpu.get_barrier_semaphore()
    for mr, mc in sorted(order, reverse=True):
        pr, pc = peer(mr, mc)
        pl.semaphore_signal(barrier, inc=1, device_id=(pc, pr), device_id_type=MESH)
    bag_load.wait()
    tile_bags = own_bags // per_vreg
    packed[...] = jnp.concatenate(
        [bags_v[q * tile_bags:(q + 1) * tile_bags, :] for q in range(per_vreg)], axis=1
    )
    gathered[r] = packed[...]
    load.wait()
    pl.semaphore_wait(barrier, len(order))

    bag_copies = []
    for mr in range(1, rows):
        pr, _ = peer(mr, 0)
        copy = pltpu.make_async_remote_copy(
            src_ref=packed, dst_ref=gathered.at[r],
            send_sem=bag_send.at[mr], recv_sem=bag_recv.at[mr],
            device_id=(c, pr), device_id_type=MESH,
        )
        copy.start()
        bag_copies.append(copy)

    copies = []

    def send(first, last):
        for i in range(first, last):
            mr, mc = order[i]
            pr, pc = peer(mr, mc)
            send_one(i, pr, pc)

    def send_one(i, pr, pc):
        copy = pltpu.make_async_remote_copy(
            src_ref=table_v.at[pl.ds((pc * rows + pr) * span, span), :],
            dst_ref=out_ref.at[r, c],
            send_sem=send_sem.at[i], recv_sem=recv_sem.at[i],
            device_id=(pc, pr), device_id_type=MESH,
        )
        copy.start()
        copies.append(copy)

    send(0, cuts[0])

    for copy in bag_copies:
        copy.wait()

    chunk = math.gcd(block_len, 16 * LANES)
    lanes = lax.broadcasted_iota(jnp.int32, (tile_bags, chunk), 1)

    def count(group, _):
        shifted = gathered[group] - r * block_len
        for q in range(per_vreg):
            at = group * own_bags + q * tile_bags
            for part in range(block_len // chunk):
                here = shifted - part * chunk
                total = jnp.zeros((tile_bags, chunk), jnp.float32)
                for l in range(bag_len):
                    lane = q * bag_len + l
                    total += jnp.where(here[:, lane:lane + 1] == lanes, 1.0, 0.0)
                counts[pl.ds(at, tile_bags), part * chunk:(part + 1) * chunk] = total
        return 0

    lax.fori_loop(0, rows, count, 0)
    send(cuts[0], cuts[1])

    depth = math.gcd(block_len, 512)
    partial[...] = jnp.zeros_like(partial)

    def multiply(turn, _):
        at = pl.multiple_of(turn * depth, depth)
        block = table_v[pl.ds(at, depth), :]
        times = counts[:, pl.ds(at, depth)].astype(jnp.bfloat16)
        high = block.astype(jnp.bfloat16)
        rest = block - high.astype(jnp.float32)
        middle = rest.astype(jnp.bfloat16)
        low = (rest - middle.astype(jnp.float32)).astype(jnp.bfloat16)
        dot = functools.partial(jnp.dot, preferred_element_type=jnp.float32)
        both = dot(times, jnp.concatenate([high, middle], axis=1))
        step = (dot(times, low) + both[:, width:]) + both[:, :width]
        partial[...] += step.reshape(partial.shape)
        return 0

    lax.fori_loop(0, block_len // depth, multiply, 0)

    low, high = lax.rem(r, half), lax.div(r, half)
    sum_copies = []
    for mr in range(1, half):
        pr, _ = peer(mr, 0)
        copy = pltpu.make_async_remote_copy(
            src_ref=partial.at[:, lax.rem(pr, half)], dst_ref=arrived.at[mr],
            send_sem=sum_send.at[mr], recv_sem=sum_recv.at[mr],
            device_id=(c, pr), device_id_type=MESH,
        )
        copy.start()
        sum_copies.append(copy)
    send(cuts[1], cuts[2])

    for copy in sum_copies:
        copy.wait()
    total = partial[:, low]
    for mr in range(1, half):
        total += arrived[mr]
    halves[...] = total
    own.wait()
    other, _ = peer(half, 0)
    across = pltpu.make_async_remote_copy(
        src_ref=halves.at[1 - high], dst_ref=crossed,
        send_sem=cross_send, recv_sem=cross_recv,
        device_id=(c, other), device_id_type=MESH,
    )
    across.start()
    send(cuts[2], len(order))
    across.wait()
    pooled_ref[...] = halves[high] + crossed[...]
    for copy in copies:
        copy.wait()


CUTS = (16, 21, 26)


def per_device(column_table, bag_rows):
    rows, cols = lax.axis_size("row"), lax.axis_size("col")
    block_len, width = column_table.shape
    own_bags, bag_len = bag_rows.shape
    span = block_len // (rows * cols)
    fits = (
        width % LANES == 0 and LANES % bag_len == 0 and own_bags * bag_len == SUBLANES * LANES
        and span % SUBLANES == 0 and block_len % LANES == 0
        and rows > 1 and rows & (rows - 1) == 0 and cols & (cols - 1) == 0
    )
    if not fits:
        return general(column_table, bag_rows)
    bags = own_bags * rows
    peers = rows * cols - 1
    half = rows // 2
    dma = pltpu.SemaphoreType.DMA
    landed, sums = pl.pallas_call(
        functools.partial(kernel, rows, cols),
        out_shape=(
            jax.ShapeDtypeStruct((rows, cols, span, width), jnp.float32),
            jax.ShapeDtypeStruct((own_bags, width), jnp.float32),
        ),
        in_specs=[pl.BlockSpec(memory_space=pltpu.HBM), pl.BlockSpec(memory_space=pltpu.HBM)],
        out_specs=(pl.BlockSpec(memory_space=pltpu.VMEM), pl.BlockSpec(memory_space=pltpu.VMEM)),
        scratch_shapes=[
            pltpu.VMEM((block_len, width), jnp.float32),
            pltpu.VMEM((own_bags, bag_len), jnp.int32),
            pltpu.VMEM((SUBLANES, LANES), jnp.int32),
            pltpu.VMEM((rows, SUBLANES, LANES), jnp.int32),
            pltpu.VMEM((bags, block_len), jnp.float32),
            pltpu.VMEM((2, half, own_bags, width), jnp.float32),
            pltpu.VMEM((half, 2, own_bags, width), jnp.float32),
            pltpu.VMEM((2, own_bags, width), jnp.float32),
            pltpu.VMEM((own_bags, width), jnp.float32),
            dma, dma, dma, dma((peers,)), dma((peers,)),
            dma((rows,)), dma((rows,)), dma((half,)), dma((half,)), dma, dma,
        ],
        compiler_params=pltpu.CompilerParams(
            collective_id=0, has_side_effects=True, vmem_limit_bytes=32 * 1024 * 1024
        ),
    )(
        pltpu.with_memory_space_constraint(column_table, pltpu.HBM),
        pltpu.with_memory_space_constraint(bag_rows, pltpu.HBM),
    )
    return pl.pallas_call(
        write_out,
        out_shape=(
            jax.ShapeDtypeStruct((rows, span, width * cols), jnp.float32),
            jax.ShapeDtypeStruct((own_bags, width), jnp.float32),
        ),
        in_specs=[pl.BlockSpec(memory_space=pltpu.VMEM)] * 2,
        out_specs=(pl.BlockSpec(memory_space=pltpu.HBM), pl.BlockSpec(memory_space=pltpu.HBM)),
        scratch_shapes=[dma((cols,)), dma],
        compiler_params=pltpu.CompilerParams(vmem_limit_bytes=8 * 1024 * 1024),
    )(landed, sums)


def write_out(landed_ref, sums_ref, out_ref, pooled_ref, sems, sum_sem):
    rows, cols, _, width = landed_ref.shape
    copies = [pltpu.make_async_copy(sums_ref, pooled_ref, sum_sem)]
    for c in range(cols):
        copies.append(pltpu.make_async_copy(
            landed_ref.at[:, c], out_ref.at[:, :, c * width:(c + 1) * width], sems.at[c]
        ))
    for copy in copies:
        copy.start()
    for copy in copies:
        copy.wait()


def solution(mesh):
    return jax.shard_map(
        per_device,
        mesh=mesh,
        in_specs=(P("row", "col"), P("row", None)),
        out_specs=(P(None, ("col", "row"), None), P("row", "col")),
        check_vma=False,
    )
```

profile of v0, /device:TPU:17, one launch (start us, length us, event | category | flops | bytes accessed | tf_op | source)
XLA Modules:
  0.0 55.2 jit_solution(647431634948766555)
XLA Ops:
  0.6 53.2 %shard_map.41 = (f32[8,4,128,128]{3,2,1,0:T(8,128)S(1)}, f32[32,128]{1,0:T(8,128)S(1)}) custom-call(f32[4096,128]{1,0:T(8,128)} %table_ref.1, s32[32,32]{1,0:T(8,128)} %bags_ref.1), custom_call_target="tpu_custom_call" | custom-call | tf_op jit(solution)/shard_map/pallas_call | solution.py:247
  53.8 1.4 %shard_map.42 = (f32[8,128,512]{2,1,0:T(8,128)}, f32[32,128]{1,0:T(8,128)}) custom-call(f32[8,4,128,128]{3,2,1,0:T(8,128)S(1)} %get-tuple-element.4.landed_ref, f32[32,128]{1,0:T(8,128)S(1)} %get-tuple-element.5.sums_ref), custom_call_target="tpu_custom_call" | custom-call | tf_op jit(solution)/shard_map/pallas_call | solution.py:275
where the time goes:
time: 55.8 us; the launch traced here: 55.2 us
  Pallas kernels  54.6 us (98%)
  between operations  0.64 us (1%)
    pallas_call x1, Pallas kernels, per_device(): pl.pallas_call(functools.partial(kernel, rows, cols), out_shape=(jax.Shap...  53.2 us
    pallas_call x1, Pallas kernels, per_device(): pl.pallas_call(write_out, out_shape=(jax.ShapeDtypeStruct((rows, span, wi...  1.36 us

commit v1 on v0

--- a/solution.py
+++ b/solution.py
@@ -64,17 +64,35 @@
 def flipped(index, mask, count):
     result, bit = 0, 1
     while bit < count:
-        digit = lax.rem(lax.div(index, bit), 2)
-        result = result + (1 - digit if mask & bit else digit) * bit
+        total = lax.div(index, bit) + (mask // bit if isinstance(mask, int) else lax.div(mask, bit))
+        result = result + lax.rem(total, 2) * bit
         bit *= 2
     return result
+
+
+def orders(rows, cols):
+    step, half, across = rows // 4, rows // 2, cols // 2
+    masks = [(mr, mc) for mr in range(rows) for mc in range(cols)]
+    spread = lambda m: -((m[0] % step > 0) + (m[1] >= across))
+    first = [(3 * step, 0)]
+    second = [(3 * step + 1, 0), (3 * step + 1, 1), (3 * step, across), (3 * step, across + 1)]
+    last = (3 * step, 1)
+    near = [m for m in masks if m[0] < step and m != (0, 0)]
+    beside = [m for m in masks if step <= m[0] < half]
+    two = sorted((m for m in masks if half <= m[0] < 3 * step), key=spread)
+    three = sorted((m for m in masks if m[0] >= 3 * step), key=spread)
+    left = [m for m in three if m not in first + second + [last]]
+    inner = two + left + [last]
+    outer = two + three
+    return first, second, inner, outer, near, beside
 
 
 def kernel(
     row_groups, col_groups,
     table_ref, bags_ref, out_ref, pooled_ref,
-    table_v, bags_v, packed, gathered, counts, partial, arrived, halves, crossed,
-    load_sem, bag_sem, own_sem, send_sem, recv_sem, bag_send, bag_recv, sum_send, sum_recv, cross_send, cross_recv,
+    table_v, bags_v, gathered, counts, partial, arrived, halves, crossed,
+    load_sem, bag_sem, own_sem, pair_sem, all_sem, send_sem, recv_sem,
+    bag_send, bag_recv, sum_send, sum_recv, cross_send, cross_recv,
 ):
     rows, cols = row_groups, col_groups
     r, c = lax.axis_index("row"), lax.axis_index("col")
@@ -82,96 +100,225 @@
     span = block_len // (rows * cols)
     own_bags, bag_len = bags_ref.shape
     per_vreg = LANES // bag_len
-    flat = c * rows + r
+    half, step = rows // 2, rows // 4
+    plane = lax.div(r, step)
+    inner = (plane == 1) | (plane == 2)
+    outer = (plane == 0) | (plane == 3)
+
+    first, second, inner_order, outer_order, near, beside = orders(rows, cols)
+    masks = [(mr, mc) for mr in range(rows) for mc in range(cols)]
+    others = [m for m in masks if m != (0, 0)]
+    meets = first + [(3 * step, 1), (1, 0), (0, cols // 2)]
+
+    def peer(mask):
+        return flipped(r, mask[0], rows), flipped(c, mask[1], cols)
+
+    def at(mask):
+        pr, pc = peer(mask)
+        return pl.ds((pc * rows + pr) * span, span)
+
+    def signal(sem, mask):
+        pr, pc = peer(mask)
+        pl.semaphore_signal(sem, inc=1, device_id=(pc, pr), device_id_type=MESH)
+
+    def load(mask):
+        return pltpu.make_async_copy(
+            table_ref.at[at(mask), :], table_v.at[at(mask), :], load_sem.at[mask[0] * cols + mask[1]]
+        )
+
+    def bulk(mask):
+        pr, pc = peer(mask)
+        return pltpu.make_async_remote_copy(
+            src_ref=table_v.at[at(mask), :], dst_ref=out_ref.at[r, c],
+            send_sem=send_sem, recv_sem=recv_sem,
+            device_id=(pc, pr), device_id_type=MESH,
+        )
+
+    def send(chosen):
+        for mask in chosen:
+            bulk(mask).start()
 
     bag_load = pltpu.make_async_copy(bags_ref, bags_v, bag_sem)
     bag_load.start()
-    load = pltpu.make_async_copy(table_ref, table_v, load_sem)
-    load.start()
-    own = pltpu.make_async_copy(
-        table_ref.at[pl.ds(flat * span, span), :],
-        out_ref.at[r, c],
-        own_sem,
-    )
+    barrier = pltpu.get_barrier_semaphore()
+
+    @pl.when(inner)
+    def _():
+        for mask in meets:
+            signal(barrier, mask)
+
+    for mask in first + second:
+        load(mask).start()
+
+    @pl.when(inner)
+    def _():
+        for mask in others:
+            if mask[0] // step in (1, 2):
+                signal(barrier, mask)
+
+    @pl.when(outer)
+    def _():
+        for mask in others:
+            if mask[0] // step in (0, 3):
+                signal(barrier, mask)
+
+    for mask in inner_order + near + beside + [(0, 0)]:
+        load(mask).start()
+    own = pltpu.make_async_copy(table_ref.at[at((0, 0)), :], out_ref.at[r, c], own_sem)
     own.start()
 
-    masks = [(mr, mc) for mr in range(rows) for mc in range(cols) if (mr, mc) != (0, 0)]
-    half = rows // 2
-    far = [m for m in masks if m[0] >= half]
-    near = sorted((m for m in masks if m[0] < half), key=lambda m: -m[0])
-    far = sorted(far, key=lambda m: (m[0] >= half + half // 2, m[1], m[0]))
-    order = [m for pair in zip(far, near + [None]) for m in pair if m]
-    cuts = [len(order) * n // 31 for n in CUTS]
-
-    def peer(mr, mc):
-        return flipped(r, mr, rows), flipped(c, mc, cols)
-
-    barrier = pltpu.get_barrier_semaphore()
-    for mr, mc in sorted(order, reverse=True):
-        pr, pc = peer(mr, mc)
-        pl.semaphore_signal(barrier, inc=1, device_id=(pc, pr), device_id_type=MESH)
+    def bag(mask):
+        pr, _ = peer((mask, 0))
+        return pltpu.make_async_remote_copy(
+            src_ref=gathered.at[r], dst_ref=gathered.at[r],
+            send_sem=bag_send.at[mask], recv_sem=bag_recv.at[mask],
+            device_id=(c, pr), device_id_type=MESH,
+        )
+
+    def pair(mask, source):
+        pr, _ = peer((step, 0))
+        rows_of = pl.ds(lax.div(flipped(r, source, rows), step) * step, step)
+        return pltpu.make_async_remote_copy(
+            src_ref=gathered.at[rows_of], dst_ref=gathered.at[rows_of],
+            send_sem=bag_send.at[mask], recv_sem=bag_recv.at[mask],
+            device_id=(c, pr), device_id_type=MESH,
+        )
+
     bag_load.wait()
-    tile_bags = own_bags // per_vreg
-    packed[...] = jnp.concatenate(
-        [bags_v[q * tile_bags:(q + 1) * tile_bags, :] for q in range(per_vreg)], axis=1
-    )
-    gathered[r] = packed[...]
-    load.wait()
-    pl.semaphore_wait(barrier, len(order))
-
-    bag_copies = []
-    for mr in range(1, rows):
-        pr, _ = peer(mr, 0)
-        copy = pltpu.make_async_remote_copy(
-            src_ref=packed, dst_ref=gathered.at[r],
-            send_sem=bag_send.at[mr], recv_sem=bag_recv.at[mr],
-            device_id=(c, pr), device_id_type=MESH,
-        )
-        copy.start()
-        bag_copies.append(copy)
-
-    copies = []
-
-    def send(first, last):
-        for i in range(first, last):
-            mr, mc = order[i]
-            pr, pc = peer(mr, mc)
-            send_one(i, pr, pc)
-
-    def send_one(i, pr, pc):
-        copy = pltpu.make_async_remote_copy(
-            src_ref=table_v.at[pl.ds((pc * rows + pr) * span, span), :],
-            dst_ref=out_ref.at[r, c],
-            send_sem=send_sem.at[i], recv_sem=recv_sem.at[i],
-            device_id=(pc, pr), device_id_type=MESH,
-        )
-        copy.start()
-        copies.append(copy)
-
-    send(0, cuts[0])
-
-    for copy in bag_copies:
-        copy.wait()
-
-    chunk = math.gcd(block_len, 16 * LANES)
-    lanes = lax.broadcasted_iota(jnp.int32, (tile_bags, chunk), 1)
-
-    def count(group, _):
+    gathered[r] = jnp.concatenate(
+        [bags_v[pl.ds(q, SUBLANES, stride=per_vreg), :] for q in range(per_vreg)], axis=1
+    )
+    for mask in first + second:
+        load(mask).wait()
+
+    @pl.when(inner)
+    def _():
+        pl.semaphore_wait(barrier, len(meets))
+        bag(3 * step).start()
+        bag(1).start()
+        send(first)
+        signal(pair_sem, (3 * step, 0))
+        signal(pair_sem, (3 * step, 1))
+        pl.semaphore_wait(pair_sem, 2)
+        bag(3 * step + 1).start()
+        send(second)
+
+    tiles = block_len // LANES
+    packed_rows = SUBLANES // per_vreg
+    slot = (
+        lax.rem(lax.broadcasted_iota(jnp.int32, (SUBLANES, LANES), 0), packed_rows) * per_vreg
+        + lax.div(lax.broadcasted_iota(jnp.int32, (SUBLANES, LANES), 1), bag_len)
+    )
+    left_rows = lax.broadcasted_iota(jnp.int32, (tiles * SUBLANES, LANES), 0)
+    right_rows = lax.broadcasted_iota(jnp.int32, (LANES, LANES), 0)
+
+    def one_hot(numbers, first, against):
+        return jnp.concatenate(
+            [
+                jnp.where(numbers[k:k + 1, :] == against, 1.0, 0.0).astype(jnp.bfloat16)
+                for k in range(first, first + packed_rows)
+            ],
+            axis=1,
+        )
+
+    def enter():
+        for mask in inner_order + near + beside + [(0, 0)]:
+            load(mask).wait()
+
+        @pl.when(inner)
+        def _():
+            for mask in (1, 3 * step, 3 * step + 1):
+                bag(mask).wait_recv()
+            pl.semaphore_wait(all_sem, 1)
+            pair(step, 0).start()
+            pair(half, 3 * step).start()
+
+        @pl.when(outer)
+        def _():
+            pl.semaphore_wait(barrier, len(others))
+            signal(all_sem, (step, 0))
+            for mask in range(rows - 1, 0, -1):
+                bag(mask).start()
+
+        go(0)
+
+    def go(n):
+        @pl.when(inner)
+        def _():
+            send(stage(inner_order, beside, near, IN, n))
+
+        @pl.when(outer)
+        def _():
+            send(stage(outer_order, beside, near, OUT, n))
+
+    def count(turn, _):
+        @pl.when(turn == 1)
+        def _():
+            enter()
+
+        @pl.when(outer)
+        def _():
+            for n, mask in enumerate((1, 3 * step, 3 * step + 1)):
+                @pl.when(turn == n + 1)
+                def _():
+                    bag(mask).wait_recv()
+
+            for n, mask in ((half, step), (half + step, half)):
+                @pl.when(turn == n)
+                def _():
+                    pair(mask, mask).wait_recv()
+
+        @pl.when(inner)
+        def _():
+            for n in range(half, rows):
+                @pl.when(turn == n)
+                def _():
+                    bag(n - step).wait_recv()
+
+        @pl.when(turn == half)
+        def _():
+            go(1)
+
+        @pl.when(turn == half + step)
+        def _():
+            go(2)
+
+        mask = turn + jnp.where(turn >= half, -step, jnp.where(turn >= step, half, 0))
+        group = flipped(r, mask, rows)
         shifted = gathered[group] - r * block_len
-        for q in range(per_vreg):
-            at = group * own_bags + q * tile_bags
-            for part in range(block_len // chunk):
-                here = shifted - part * chunk
-                total = jnp.zeros((tile_bags, chunk), jnp.float32)
-                for l in range(bag_len):
-                    lane = q * bag_len + l
-                    total += jnp.where(here[:, lane:lane + 1] == lanes, 1.0, 0.0)
-                counts[pl.ds(at, tile_bags), part * chunk:(part + 1) * chunk] = total
+        tile = lax.shift_right_arithmetic(shifted, LANES.bit_length() - 1)
+        lane = shifted - tile * LANES
+        code = tile * SUBLANES + slot
+        for k in range(SUBLANES // packed_rows):
+            found = lax.dot_general(
+                one_hot(code, k * packed_rows, left_rows),
+                one_hot(lane, k * packed_rows, right_rows),
+                (((1,), (1,)), ((), ())),
+                preferred_element_type=jnp.float32,
+            )
+            row = group * own_bags + k * SUBLANES
+            for t in range(tiles):
+                counts[pl.ds(row, SUBLANES), t * LANES:(t + 1) * LANES] = (
+                    found[t * SUBLANES:(t + 1) * SUBLANES, :]
+                )
         return 0
 
     lax.fori_loop(0, rows, count, 0)
-    send(cuts[0], cuts[1])
-
+
+    @pl.when(inner)
+    def _():
+        for mask in (1, 3 * step, 3 * step + 1):
+            bag(mask).wait_send()
+        pair(step, 0).wait_send()
+        pair(half, 3 * step).wait_send()
+
+    @pl.when(outer)
+    def _():
+        for mask in range(1, rows):
+            bag(mask).wait_send()
+
+
+    go(3)
     depth = math.gcd(block_len, 512)
     partial[...] = jnp.zeros_like(partial)
 
@@ -194,7 +341,7 @@
     low, high = lax.rem(r, half), lax.div(r, half)
     sum_copies = []
     for mr in range(1, half):
-        pr, _ = peer(mr, 0)
+        pr, _ = peer((mr, 0))
         copy = pltpu.make_async_remote_copy(
             src_ref=partial.at[:, lax.rem(pr, half)], dst_ref=arrived.at[mr],
             send_sem=sum_send.at[mr], recv_sem=sum_recv.at[mr],
@@ -202,8 +349,8 @@
         )
         copy.start()
         sum_copies.append(copy)
-    send(cuts[1], cuts[2])
-
+
+    go(4)
     for copy in sum_copies:
         copy.wait()
     total = partial[:, low]
@@ -211,21 +358,36 @@
         total += arrived[mr]
     halves[...] = total
     own.wait()
-    other, _ = peer(half, 0)
+    other, _ = peer((half, 0))
     across = pltpu.make_async_remote_copy(
         src_ref=halves.at[1 - high], dst_ref=crossed,
         send_sem=cross_send, recv_sem=cross_recv,
         device_id=(c, other), device_id_type=MESH,
     )
     across.start()
-    send(cuts[2], len(order))
+
+    go(5)
     across.wait()
+    go(6)
     pooled_ref[...] = halves[high] + crossed[...]
-    for copy in copies:
-        copy.wait()
-
-
-CUTS = (16, 21, 26)
+    moved = pl.ds(0, len(others) * span)
+    for sem in (send_sem, recv_sem):
+        pltpu.make_async_copy(table_ref.at[moved, :], table_v.at[moved, :], sem).wait()
+
+
+def stage(far, beside, near, cuts, n):
+    def part(chosen, ends):
+        ends = (0,) + ends + (len(chosen),)
+        return chosen[ends[n]:ends[n + 1]]
+
+    one, two, three = part(far, cuts[0]), part(beside, cuts[1]), part(near, cuts[2])
+    result = []
+    for k in range(max(len(one), len(two))):
+        result += two[k:k + 1] + one[k:k + 1]
+    return result + three
+
+
+IN, OUT = ((1, 2, 3, 4, 5, 6), (1, 2, 3, 4, 5, 6), (0, 0, 0, 0, 0, 0)), ((2, 3, 4, 5, 6, 7), (1, 2, 3, 4, 5, 6), (0, 0, 0, 0, 0, 0))
 
 
 def per_device(column_table, bag_rows):
@@ -234,14 +396,13 @@
     own_bags, bag_len = bag_rows.shape
     span = block_len // (rows * cols)
     fits = (
-        width % LANES == 0 and LANES % bag_len == 0 and own_bags * bag_len == SUBLANES * LANES
+        width % LANES == 0 and LANES % bag_len == 0 and bag_len * SUBLANES >= LANES and own_bags * bag_len == SUBLANES * LANES
         and span % SUBLANES == 0 and block_len % LANES == 0
-        and rows > 1 and rows & (rows - 1) == 0 and cols & (cols - 1) == 0
+        and rows // 4 == 2 and rows % 4 == 0 and cols >= 4 and cols & (cols - 1) == 0
     )
     if not fits:
         return general(column_table, bag_rows)
     bags = own_bags * rows
-    peers = rows * cols - 1
     half = rows // 2
     dma = pltpu.SemaphoreType.DMA
     landed, sums = pl.pallas_call(
@@ -255,15 +416,17 @@
         scratch_shapes=[
             pltpu.VMEM((block_len, width), jnp.float32),
             pltpu.VMEM((own_bags, bag_len), jnp.int32),
-            pltpu.VMEM((SUBLANES, LANES), jnp.int32),
             pltpu.VMEM((rows, SUBLANES, LANES), jnp.int32),
             pltpu.VMEM((bags, block_len), jnp.float32),
             pltpu.VMEM((2, half, own_bags, width), jnp.float32),
             pltpu.VMEM((half, 2, own_bags, width), jnp.float32),
             pltpu.VMEM((2, own_bags, width), jnp.float32),
             pltpu.VMEM((own_bags, width), jnp.float32),
-            dma, dma, dma, dma((peers,)), dma((peers,)),
-            dma((rows,)), dma((rows,)), dma((half,)), dma((half,)), dma, dma,
+            dma((rows * cols,)), dma, dma,
+            pltpu.SemaphoreType.REGULAR, pltpu.SemaphoreType.REGULAR,
+            dma, dma,
+            dma((rows,)), dma((rows,)),
+            dma((half,)), dma((half,)), dma, dma,
         ],
         compiler_params=pltpu.CompilerParams(
             collective_id=0, has_side_effects=True, vmem_limit_bytes=32 * 1024 * 1024

time: 55.8 us -> 55.1 us (0.987)
  no operation moved by 1% of the time
where the time goes in v1:
time: 55.1 us; the launch traced here: 54.8 us
  Pallas kernels  54.2 us (98%)
  between operations  0.64 us (1%)
    pallas_call x1, Pallas kernels, per_device(): pl.pallas_call(functools.partial(kernel, rows, cols), out_shape=(jax.Shap...  52.8 us
    pallas_call x1, Pallas kernels, per_device(): pl.pallas_call(write_out, out_shape=(jax.ShapeDtypeStruct((rows, span, wi...  1.36 us

profile of v1, /device:TPU:17, one launch (start us, length us, event | category | flops | bytes accessed | tf_op | source)
XLA Modules:
  0.0 54.8 jit_solution(9296211131189679008)
XLA Ops:
  0.6 52.8 %shard_map.41 = (f32[8,4,128,128]{3,2,1,0:T(8,128)S(1)}, f32[32,128]{1,0:T(8,128)S(1)}) custom-call(f32[4096,128]{1,0:T(8,128)} %table_ref.1, s32[32,32]{1,0:T(8,128)} %bags_ref.1), custom_call_target="tpu_custom_call" | custom-call | tf_op jit(solution)/shard_map/pallas_call | solution.py:408
  53.5 1.4 %shard_map.42 = (f32[8,128,512]{2,1,0:T(8,128)}, f32[32,128]{1,0:T(8,128)}) custom-call(f32[8,4,128,128]{3,2,1,0:T(8,128)S(1)} %get-tuple-element.4.landed_ref, f32[32,128]{1,0:T(8,128)S(1)} %get-tuple-element.5.sums_ref), custom_call_target="tpu_custom_call" | custom-call | tf_op jit(solution)/shard_map/pallas_call | solution.py:438

commit v2 on v1

--- a/solution.py
+++ b/solution.py
@@ -121,10 +121,13 @@
         pr, pc = peer(mask)
         pl.semaphore_signal(sem, inc=1, device_id=(pc, pr), device_id_type=MESH)
 
-    def load(mask):
-        return pltpu.make_async_copy(
-            table_ref.at[at(mask), :], table_v.at[at(mask), :], load_sem.at[mask[0] * cols + mask[1]]
-        )
+    def load(chosen, sem):
+        for mask in chosen:
+            pltpu.make_async_copy(table_ref.at[at(mask), :], table_v.at[at(mask), :], sem).start()
+
+    def chunks(count, sem):
+        whole = pl.ds(0, count * span)
+        pltpu.make_async_copy(table_ref.at[whole, :], table_v.at[whole, :], sem).wait()
 
     def bulk(mask):
         pr, pc = peer(mask)
@@ -147,8 +150,8 @@
         for mask in meets:
             signal(barrier, mask)
 
-    for mask in first + second:
-        load(mask).start()
+    load(first, load_sem.at[0])
+    load(second, load_sem.at[1])
 
     @pl.when(inner)
     def _():
@@ -162,45 +165,53 @@
             if mask[0] // step in (0, 3):
                 signal(barrier, mask)
 
-    for mask in inner_order + near + beside + [(0, 0)]:
-        load(mask).start()
+    rest = inner_order + near + beside + [(0, 0)]
+    load(rest, load_sem.at[2])
     own = pltpu.make_async_copy(table_ref.at[at((0, 0)), :], out_ref.at[r, c], own_sem)
     own.start()
 
-    def bag(mask):
+    def bag(mask, kind):
         pr, _ = peer((mask, 0))
         return pltpu.make_async_remote_copy(
             src_ref=gathered.at[r], dst_ref=gathered.at[r],
-            send_sem=bag_send.at[mask], recv_sem=bag_recv.at[mask],
+            send_sem=bag_send, recv_sem=bag_recv.at[kind],
             device_id=(c, pr), device_id_type=MESH,
         )
 
-    def pair(mask, source):
+    def pair(source):
+        kind = 1
         pr, _ = peer((step, 0))
         rows_of = pl.ds(lax.div(flipped(r, source, rows), step) * step, step)
         return pltpu.make_async_remote_copy(
             src_ref=gathered.at[rows_of], dst_ref=gathered.at[rows_of],
-            send_sem=bag_send.at[mask], recv_sem=bag_recv.at[mask],
+            send_sem=bag_send, recv_sem=bag_recv.at[kind],
             device_id=(c, pr), device_id_type=MESH,
         )
+
+    def bags(count, sem):
+        whole = gathered.at[pl.ds(0, count)]
+        pltpu.make_async_remote_copy(
+            src_ref=whole, dst_ref=whole, send_sem=bag_send, recv_sem=sem,
+            device_id=peer((1, 0))[::-1], device_id_type=MESH,
+        ).wait_recv()
 
     bag_load.wait()
     gathered[r] = jnp.concatenate(
         [bags_v[pl.ds(q, SUBLANES, stride=per_vreg), :] for q in range(per_vreg)], axis=1
     )
-    for mask in first + second:
-        load(mask).wait()
+    chunks(len(first), load_sem.at[0])
 
     @pl.when(inner)
     def _():
         pl.semaphore_wait(barrier, len(meets))
-        bag(3 * step).start()
-        bag(1).start()
+        bag(3 * step, 0).start()
+        bag(1, 0).start()
         send(first)
         signal(pair_sem, (3 * step, 0))
         signal(pair_sem, (3 * step, 1))
+        chunks(len(second), load_sem.at[1])
         pl.semaphore_wait(pair_sem, 2)
-        bag(3 * step + 1).start()
+        bag(3 * step + 1, 0).start()
         send(second)
 
     tiles = block_len // LANES
@@ -222,23 +233,22 @@
         )
 
     def enter():
-        for mask in inner_order + near + beside + [(0, 0)]:
-            load(mask).wait()
+        chunks(len(rest), load_sem.at[2])
 
         @pl.when(inner)
         def _():
-            for mask in (1, 3 * step, 3 * step + 1):
-                bag(mask).wait_recv()
+            bags(half - 1, bag_recv.at[0])
             pl.semaphore_wait(all_sem, 1)
-            pair(step, 0).start()
-            pair(half, 3 * step).start()
+            pair(0).start()
+            pair(3 * step).start()
 
         @pl.when(outer)
         def _():
+            chunks(len(second), load_sem.at[1])
             pl.semaphore_wait(barrier, len(others))
             signal(all_sem, (step, 0))
             for mask in range(rows - 1, 0, -1):
-                bag(mask).start()
+                bag(mask, 0 if mask < step or mask >= 3 * step else 1).start()
 
         go(0)
 
@@ -256,27 +266,13 @@
         def _():
             enter()
 
-        @pl.when(outer)
-        def _():
-            for n, mask in enumerate((1, 3 * step, 3 * step + 1)):
-                @pl.when(turn == n + 1)
-                def _():
-                    bag(mask).wait_recv()
-
-            for n, mask in ((half, step), (half + step, half)):
-                @pl.when(turn == n)
-                def _():
-                    pair(mask, mask).wait_recv()
-
-        @pl.when(inner)
-        def _():
-            for n in range(half, rows):
-                @pl.when(turn == n)
-                def _():
-                    bag(n - step).wait_recv()
+        @pl.when((turn == 1) & outer)
+        def _():
+            bags(half - 1, bag_recv.at[0])
 
         @pl.when(turn == half)
         def _():
+            bags(half, bag_recv.at[1])
             go(1)
 
         @pl.when(turn == half + step)
@@ -305,18 +301,7 @@
 
     lax.fori_loop(0, rows, count, 0)
 
-    @pl.when(inner)
-    def _():
-        for mask in (1, 3 * step, 3 * step + 1):
-            bag(mask).wait_send()
-        pair(step, 0).wait_send()
-        pair(half, 3 * step).wait_send()
-
-    @pl.when(outer)
-    def _():
-        for mask in range(1, rows):
-            bag(mask).wait_send()
-
+    bags(rows - 1, bag_send)
 
     go(3)
     depth = math.gcd(block_len, 512)
@@ -339,20 +324,18 @@
     lax.fori_loop(0, block_len // depth, multiply, 0)
 
     low, high = lax.rem(r, half), lax.div(r, half)
-    sum_copies = []
     for mr in range(1, half):
         pr, _ = peer((mr, 0))
         copy = pltpu.make_async_remote_copy(
             src_ref=partial.at[:, lax.rem(pr, half)], dst_ref=arrived.at[mr],
-            send_sem=sum_send.at[mr], recv_sem=sum_recv.at[mr],
+            send_sem=sum_send, recv_sem=sum_recv,
             device_id=(c, pr), device_id_type=MESH,
         )
         copy.start()
-        sum_copies.append(copy)
 
     go(4)
-    for copy in sum_copies:
-        copy.wait()
+    for sem in (sum_send, sum_recv):
+        pltpu.make_async_copy(arrived.at[pl.ds(1, half - 1)], arrived.at[pl.ds(1, half - 1)], sem).wait()
     total = partial[:, low]
     for mr in range(1, half):
         total += arrived[mr]
@@ -387,7 +370,8 @@
     return result + three
 
 
-IN, OUT = ((1, 2, 3, 4, 5, 6), (1, 2, 3, 4, 5, 6), (0, 0, 0, 0, 0, 0)), ((2, 3, 4, 5, 6, 7), (1, 2, 3, 4, 5, 6), (0, 0, 0, 0, 0, 0))
+IN = (5, 5, 5, 5, 5, 11), (0, 0, 0, 0, 8, 8), (0, 0, 0, 0, 0, 7)
+OUT = (0, 0, 0, 0, 4, 16), (2, 2, 2, 2, 4, 8), (3, 3, 3, 3, 7, 7)
 
 
 def per_device(column_table, bag_rows):
@@ -422,11 +406,10 @@
             pltpu.VMEM((half, 2, own_bags, width), jnp.float32),
             pltpu.VMEM((2, own_bags, width), jnp.float32),
             pltpu.VMEM((own_bags, width), jnp.float32),
-            dma((rows * cols,)), dma, dma,
+            dma((3,)), dma, dma,
             pltpu.SemaphoreType.REGULAR, pltpu.SemaphoreType.REGULAR,
             dma, dma,
-            dma((rows,)), dma((rows,)),
-            dma((half,)), dma((half,)), dma, dma,
+            dma, dma((2,)), dma, dma, dma, dma,
         ],
         compiler_params=pltpu.CompilerParams(
             collective_id=0, has_side_effects=True, vmem_limit_bytes=32 * 1024 * 1024

time: 55.1 us -> 52.8 us (0.958)
  Pallas kernels: 54.2 us -> 51.8 us
    pallas_call x1, Pallas kernels: 52.8 us -> 50.4 us  [per_device(): pl.pallas_call(functools.partial(kernel, rows, cols), out_shape=(jax.Shap...]
where the time goes in v2:
time: 52.8 us; the launch traced here: 52.4 us
  Pallas kernels  51.8 us (98%)
  between operations  0.64 us (1%)
    pallas_call x1, Pallas kernels, per_device(): pl.pallas_call(functools.partial(kernel, rows, cols), out_shape=(jax.Shap...  50.4 us
    pallas_call x1, Pallas kernels, per_device(): pl.pallas_call(write_out, out_shape=(jax.ShapeDtypeStruct((rows, span, wi...  1.36 us

profile of v2, /device:TPU:17, one launch (start us, length us, event | category | flops | bytes accessed | tf_op | source)
XLA Modules:
  0.0 52.4 jit_solution(15921762529234697395)
XLA Ops:
  0.6 50.4 %shard_map.41 = (f32[8,4,128,128]{3,2,1,0:T(8,128)S(1)}, f32[32,128]{1,0:T(8,128)S(1)}) custom-call(f32[4096,128]{1,0:T(8,128)} %table_ref.1, s32[32,32]{1,0:T(8,128)} %bags_ref.1), custom_call_target="tpu_custom_call" | custom-call | tf_op jit(solution)/shard_map/pallas_call | solution.py:392
  51.1 1.4 %shard_map.42 = (f32[8,128,512]{2,1,0:T(8,128)}, f32[32,128]{1,0:T(8,128)}) custom-call(f32[8,4,128,128]{3,2,1,0:T(8,128)S(1)} %get-tuple-element.4.landed_ref, f32[32,128]{1,0:T(8,128)S(1)} %get-tuple-element.5.sums_ref), custom_call_target="tpu_custom_call" | custom-call | tf_op jit(solution)/shard_map/pallas_call | solution.py:421

commit v3 on v2

--- a/solution.py
+++ b/solution.py
@@ -82,9 +82,9 @@
     two = sorted((m for m in masks if half <= m[0] < 3 * step), key=spread)
     three = sorted((m for m in masks if m[0] >= 3 * step), key=spread)
     left = [m for m in three if m not in first + second + [last]]
-    inner = two + left + [last]
-    outer = two + three
-    return first, second, inner, outer, near, beside
+    mixed = [m for pair in zip(two, three) for m in pair]
+    far = [mixed, two + left + [last], two + left + [last], two + three]
+    return first, second, far, near, beside
 
 
 def kernel(
@@ -105,10 +105,10 @@
     inner = (plane == 1) | (plane == 2)
     outer = (plane == 0) | (plane == 3)
 
-    first, second, inner_order, outer_order, near, beside = orders(rows, cols)
+    first, second, far, near, beside = orders(rows, cols)
     masks = [(mr, mc) for mr in range(rows) for mc in range(cols)]
     others = [m for m in masks if m != (0, 0)]
-    meets = first + [(3 * step, 1), (1, 0), (0, cols // 2)]
+    meets = [(3 * step, 0), (3 * step, 1), (1, 0), (0, cols // 2)]
 
     def peer(mask):
         return flipped(r, mask[0], rows), flipped(c, mask[1], cols)
@@ -165,7 +165,7 @@
             if mask[0] // step in (0, 3):
                 signal(barrier, mask)
 
-    rest = inner_order + near + beside + [(0, 0)]
+    rest = far[1] + near + beside + [(0, 0)]
     load(rest, load_sem.at[2])
     own = pltpu.make_async_copy(table_ref.at[at((0, 0)), :], out_ref.at[r, c], own_sem)
     own.start()
@@ -253,13 +253,10 @@
         go(0)
 
     def go(n):
-        @pl.when(inner)
-        def _():
-            send(stage(inner_order, beside, near, IN, n))
-
-        @pl.when(outer)
-        def _():
-            send(stage(outer_order, beside, near, OUT, n))
+        for place in range(4):
+            @pl.when(plane == place)
+            def _():
+                send(stage(far[place], beside, near, CUTS[place], n))
 
     def count(turn, _):
         @pl.when(turn == 1)
@@ -334,8 +331,8 @@
         copy.start()
 
     go(4)
-    for sem in (sum_send, sum_recv):
-        pltpu.make_async_copy(arrived.at[pl.ds(1, half - 1)], arrived.at[pl.ds(1, half - 1)], sem).wait()
+    sent = arrived.at[pl.ds(1, half - 1)]
+    pltpu.make_async_copy(sent, sent, sum_recv).wait()
     total = partial[:, low]
     for mr in range(1, half):
         total += arrived[mr]
@@ -353,6 +350,7 @@
     across.wait()
     go(6)
     pooled_ref[...] = halves[high] + crossed[...]
+    pltpu.make_async_copy(sent, sent, sum_send).wait()
     moved = pl.ds(0, len(others) * span)
     for sem in (send_sem, recv_sem):
         pltpu.make_async_copy(table_ref.at[moved, :], table_v.at[moved, :], sem).wait()
@@ -364,14 +362,14 @@
         return chosen[ends[n]:ends[n + 1]]
 
     one, two, three = part(far, cuts[0]), part(beside, cuts[1]), part(near, cuts[2])
-    result = []
-    for k in range(max(len(one), len(two))):
-        result += two[k:k + 1] + one[k:k + 1]
+    spread = [((k + 0.5) / len(chosen), m) for chosen in (two, one) for k, m in enumerate(chosen)]
+    result = [m for _, m in sorted(spread, key=lambda p: p[0])]
     return result + three
 
 
-IN = (5, 5, 5, 5, 5, 11), (0, 0, 0, 0, 8, 8), (0, 0, 0, 0, 0, 7)
-OUT = (0, 0, 0, 0, 4, 16), (2, 2, 2, 2, 4, 8), (3, 3, 3, 3, 7, 7)
+INNER = (5, 5, 5, 5, 5, 11), (1, 1, 1, 1, 8, 8), (0, 0, 0, 0, 0, 7)
+OUTER = (0, 0, 0, 0, 4, 16), (2, 2, 2, 2, 4, 8), (3, 3, 3, 3, 7, 7)
+CUTS = OUTER, INNER, INNER, OUTER
 
 
 def per_device(column_table, bag_rows):

time: 52.8 us -> 52.8 us (level)
  no operation moved by 1% of the time
where the time goes in v3:
time: 52.8 us; the launch traced here: 52.6 us
  Pallas kernels  51.9 us (98%)
  between operations  0.64 us (1%)
    pallas_call x1, Pallas kernels, per_device(): pl.pallas_call(functools.partial(kernel, rows, cols), out_shape=(jax.Shap...  50.6 us
    pallas_call x1, Pallas kernels, per_device(): pl.pallas_call(write_out, out_shape=(jax.ShapeDtypeStruct((rows, span, wi...  1.36 us

profile of v3, /device:TPU:17, one launch (start us, length us, event | category | flops | bytes accessed | tf_op | source)
XLA Modules:
  0.0 52.6 jit_solution(12745106034307450373)
XLA Ops:
  0.6 50.6 %shard_map.41 = (f32[8,4,128,128]{3,2,1,0:T(8,128)S(1)}, f32[32,128]{1,0:T(8,128)S(1)}) custom-call(f32[4096,128]{1,0:T(8,128)} %table_ref.1, s32[32,32]{1,0:T(8,128)} %bags_ref.1), custom_call_target="tpu_custom_call" | custom-call | tf_op jit(solution)/shard_map/pallas_call | solution.py:390
  51.2 1.4 %shard_map.42 = (f32[8,128,512]{2,1,0:T(8,128)}, f32[32,128]{1,0:T(8,128)}) custom-call(f32[8,4,128,128]{3,2,1,0:T(8,128)S(1)} %get-tuple-element.4.landed_ref, f32[32,128]{1,0:T(8,128)S(1)} %get-tuple-element.5.sums_ref), custom_call_target="tpu_custom_call" | custom-call | tf_op jit(solution)/shard_map/pallas_call | solution.py:419

commit v4 on v2

--- a/solution.py
+++ b/solution.py
@@ -141,8 +141,6 @@
         for mask in chosen:
             bulk(mask).start()
 
-    bag_load = pltpu.make_async_copy(bags_ref, bags_v, bag_sem)
-    bag_load.start()
     barrier = pltpu.get_barrier_semaphore()
 
     @pl.when(inner)
@@ -150,6 +148,8 @@
         for mask in meets:
             signal(barrier, mask)
 
+    bag_load = pltpu.make_async_copy(bags_ref, bags_v, bag_sem)
+    bag_load.start()
     load(first, load_sem.at[0])
     load(second, load_sem.at[1])
 
@@ -205,8 +205,8 @@
     def _():
         pl.semaphore_wait(barrier, len(meets))
         bag(3 * step, 0).start()
+        send(first)
         bag(1, 0).start()
-        send(first)
         signal(pair_sem, (3 * step, 0))
         signal(pair_sem, (3 * step, 1))
         chunks(len(second), load_sem.at[1])
@@ -426,22 +426,21 @@
         ),
         in_specs=[pl.BlockSpec(memory_space=pltpu.VMEM)] * 2,
         out_specs=(pl.BlockSpec(memory_space=pltpu.HBM), pl.BlockSpec(memory_space=pltpu.HBM)),
-        scratch_shapes=[dma((cols,)), dma],
+        scratch_shapes=[dma, dma],
         compiler_params=pltpu.CompilerParams(vmem_limit_bytes=8 * 1024 * 1024),
     )(landed, sums)
 
 
-def write_out(landed_ref, sums_ref, out_ref, pooled_ref, sems, sum_sem):
-    rows, cols, _, width = landed_ref.shape
-    copies = [pltpu.make_async_copy(sums_ref, pooled_ref, sum_sem)]
+def write_out(landed_ref, sums_ref, out_ref, pooled_ref, sem, sum_sem):
+    cols, width = landed_ref.shape[1], landed_ref.shape[3]
     for c in range(cols):
-        copies.append(pltpu.make_async_copy(
-            landed_ref.at[:, c], out_ref.at[:, :, c * width:(c + 1) * width], sems.at[c]
-        ))
-    for copy in copies:
-        copy.start()
-    for copy in copies:
-        copy.wait()
+        pltpu.make_async_copy(
+            landed_ref.at[:, c], out_ref.at[:, :, c * width:(c + 1) * width], sem
+        ).start()
+    pooled = pltpu.make_async_copy(sums_ref, pooled_ref, sum_sem)
+    pooled.start()
+    pooled.wait()
+    pltpu.make_async_copy(out_ref, out_ref, sem).wait()
 
 
 def solution(mesh):

time: 52.8 us -> 52.8 us (level)
  no operation moved by 1% of the time
where the time goes in v4:
time: 52.8 us; the launch traced here: 52.4 us
  Pallas kernels  51.7 us (98%)
  between operations  0.64 us (1%)
    pallas_call x1, Pallas kernels, per_device(): pl.pallas_call(functools.partial(kernel, rows, cols), out_shape=(jax.Shap...  50.4 us
    pallas_call x1, Pallas kernels, per_device(): pl.pallas_call(write_out, out_shape=(jax.ShapeDtypeStruct((rows, span, wi...  1.33 us

profile of v4, /device:TPU:17, one launch (start us, length us, event | category | flops | bytes accessed | tf_op | source)
XLA Modules:
  0.0 52.4 jit_solution(17633591052579834451)
XLA Ops:
  0.6 50.4 %shard_map.41 = (f32[8,4,128,128]{3,2,1,0:T(8,128)S(1)}, f32[32,128]{1,0:T(8,128)S(1)}) custom-call(f32[4096,128]{1,0:T(8,128)} %table_ref.1, s32[32,32]{1,0:T(8,128)} %bags_ref.1), custom_call_target="tpu_custom_call" | custom-call | tf_op jit(solution)/shard_map/pallas_call | solution.py:392
  51.0 1.3 %shard_map.42 = (f32[8,128,512]{2,1,0:T(8,128)}, f32[32,128]{1,0:T(8,128)}) custom-call(f32[8,4,128,128]{3,2,1,0:T(8,128)S(1)} %get-tuple-element.4.landed_ref, f32[32,128]{1,0:T(8,128)S(1)} %get-tuple-element.5.sums_ref), custom_call_target="tpu_custom_call" | custom-call | tf_op jit(solution)/shard_map/pallas_call | solution.py:421
